TPU v7x, 8 devices: a whole 2x2x1 slice. The times are simulated.
8 devices in a mesh: data: 1 (over z), time: 8 (over y, x, core).
Axes of the slice: x: 2, y: 2, z: 1, core: 2. Of those that a mesh axis runs over, the one named last changes fastest.
Arguments:
- x_init: float32 [32, 16, 256], P('data')
- w_in: bfloat16 [256, 1024], replicated
- w_out: bfloat16 [1024, 256], replicated
- gamma_c: bfloat16 [48, 1024], P('time')
- beta_c: bfloat16 [48, 1024], P('time')
- gamma_u: bfloat16 [48, 1024], P('time')
- beta_u: bfloat16 [48, 1024], P('time')
- step_h: float32 [48], P('time')
- guide_w: float32 [1], replicated
Outputs:
- output: float32 [48, 32, 16, 256], P('time', 'data')
All inputs are finite; a program needn't handle non-finite values.
Results may differ from a plain program's by a relative error of at most 0.00827.
Values are sent between devices in bfloat16 or wider.
A program may use at most 1 GiB of HBM per device.

v0:
```python
import jax
import jax.numpy as jnp
import math
from jax import lax
from jax.sharding import PartitionSpec as P

NUM_SWEEPS = 4


def solution(mesh):
    num_time = mesh.shape["time"]
    num_levels = math.ceil(math.log2(num_time))
    shift_perms = [[(src, src + 2 ** level) for src in range(num_time - 2 ** level)] for level in range(num_levels)]

    def local(x_init, w_in, w_out, gamma_c, beta_c, gamma_u, beta_u, step_h, guide_w):
        guide = guide_w[0]
        gain_pair = 1.0 + jnp.stack([gamma_c, gamma_u], axis=0).astype(jnp.float32)
        shift_pair = jnp.stack([beta_c, beta_u], axis=0).astype(jnp.float32)

        def sweep(index, states):
            pre_act = jnp.einsum("kbnc,cd->kbnd", states.astype(jnp.bfloat16), w_in, preferred_element_type=jnp.float32)
            act = jax.nn.gelu(pre_act[None] * gain_pair[:, :, None, None, :] + shift_pair[:, :, None, None, :]).astype(jnp.bfloat16)
            outs = jnp.einsum("ekbnd,dc->ekbnc", act, w_out, preferred_element_type=jnp.float32)
            drift = step_h[:, None, None, None] * ((1.0 + guide) * outs[0] - guide * outs[1])
            running = jnp.cumsum(drift, axis=0)
            dev_total = running[-1]
            prefix = dev_total
            for perm in shift_perms:
                prefix = prefix + lax.ppermute(prefix, "time", perm)
            before = prefix - dev_total
            local_before = jnp.concatenate([jnp.zeros_like(drift[:1]), running[:-1]], axis=0)
            return x_init[None] + (before[None] + local_before)

        start = jnp.broadcast_to(x_init[None], (step_h.shape[0],) + x_init.shape)
        return lax.fori_loop(0, NUM_SWEEPS, sweep, start)

    return jax.shard_map(local, mesh=mesh, in_specs=(P("data", None, None), P(None, None), P(None, None), P("time", None), P("time", None), P("time", None), P("time", None), P("time"), P(None)), out_specs=P("time", "data", None, None), check_vma=False)
```

profile of v0, /device:TPU:0, one launch (start us, length us, event | category | flops | bytes accessed | tf_op | source)
XLA Modules:
  0.0 239.3 jit_solution(9378977129428244566)
XLA Ops:
  0.7 0.7 convert_add_fusion
  1.4 0.7 maximum_convert_fusion
  2.2 1.4 broadcast_in_dim.2
  3.6 234.0 %while.11 = (s32[]{:T(128)}, f32[6,32,16,256]{3,2,1,0:T(8,128)S(1)}, f32[32,16,256]{2,1,0:T(8,128)}, f32[6]{0:T(128)S(1)}, f32[]{:T(128)}, /*index=5*/bf16[256,1...) while((s32[]{:T(128)}, ...), condition=%wide.region_2.3_spmd, body=%wide.region_0.2_spmd.sunk | while | flops 4911005696 | bytes 71926048 | solution.py:35
  3.6 0.0 copy-start.2
  3.6 2.9 %fusion.41 = f32[6,32,16,1024]{3,2,1,0:T(8,128)S(1)} fusion(f32[6,32,16,256]{3,2,1,0:T(8,128)S(1)} %get-tuple-element.187, bf16[256,1024]{1,0:T(8,128)(2,1)} %get-tuple-element.202), kind=kOutput, calls=%fused_computation.18.clone.1 | convolution fusion | flops 1611399168 | bytes 16252928 | tf_op jit(solution)/shard_map/while/body/eval_jaxpr/kbnc,cd->kbnd/dot_general | solution.py:21
  6.6 10.5 %fusion.42 = f32[2,6,32,16,256]{4,3,2,1,0:T(8,128)S(1)} fusion(f32[2,6,1024]{2,1,0:T(8,128)S(1)} %get-tuple-element.204, f32[2,6,1024]{2,1,0:T(8,128)S(1)} %get-tuple-element.203, f32[6,32,16,1024]{3,2,1,0:T(8,128)S(1)} %fusion.41, bf16[1024,256]{1,0:T(8,128)(2,1)S(1)} %copy-done.2), kind=kOutput, calls=%fused_computation.9.clone.1 | convolution fusion | flops 3290431488 | bytes 19496960 | tf_op jit(solution)/shard_map/while/body/eval_jaxpr/ekbnd,dc->ekbnc/dot_general | solution.py:23
  17.1 1.5 fusion.43
  18.7 2.8 %collective-permute-start = (f32[32,16,256]{2,1,0:T(8,128)S(1)}, f32[32,16,256]{2,1,0:T(8,128)S(1)}, u32[]{:S(2)}, u32[]{:S(2)}) collective-permute-start(f32[32,16,256]{2,1,0:T(8,128)S(1)} %slice_bitcast_fusion.2), channel_id=1, source_target_pairs={{0,1},{1,2},{2,3},{3,4},{4,5},{5,6},{6,7}} | collective-permute-start | bytes 1572872 | tf_op jit(solution)/shard_map/while/body/eval_jaxpr/ppermute | solution.py:29
  21.5 1.5 collective-permute-done
  22.9 0.1 fusion.44
  23.0 11.5 %collective-permute-start.1 = (f32[32,16,256]{2,1,0:T(8,128)S(1)}, f32[32,16,256]{2,1,0:T(8,128)S(1)}, u32[]{:S(2)}, u32[]{:S(2)}) collective-permute-start(f32[32,16,256]{2,1,0:T(8,128)S(1)} %fusion.44), channel_id=1, source_target_pairs={{0,2},{1,3},{2,4},{3,5},{4,6},{5,7}} | collective-permute-start | bytes 1572872 | tf_op jit(solution)/shard_map/while/body/eval_jaxpr/ppermute | solution.py:29
  34.5 10.4 %collective-permute-done.1 = f32[32,16,256]{2,1,0:T(8,128)S(1)} collective-permute-done((f32[32,16,256]{2,1,0:T(8,128)S(1)}, f32[32,16,256]{2,1,0:T(8,128)S(1)}, u32[]{:S(2)}, u32[]{:S(2)}) %collective-permute-start.1) | collective-permute-done | bytes 524320 | tf_op jit(solution)/shard_map/while/body/eval_jaxpr/ppermute | solution.py:29
  44.9 0.9 add.127
  45.8 6.4 %collective-permute-start.2 = (f32[32,16,256]{2,1,0:T(8,128)}, f32[32,16,256]{2,1,0:T(8,128)}, u32[]{:S(2)}, u32[]{:S(2)}) collective-permute-start(f32[32,16,256]{2,1,0:T(8,128)} %add.127), channel_id=1, source_target_pairs={{0,4},{1,5},{2,6},{3,7}} | collective-permute-start | bytes 1572872 | tf_op jit(solution)/shard_map/while/body/eval_jaxpr/ppermute | solution.py:29
  52.2 1.7 slice.48
  53.9 5.8 %collective-permute-done.2 = f32[32,16,256]{2,1,0:T(8,128)} collective-permute-done((f32[32,16,256]{2,1,0:T(8,128)}, f32[32,16,256]{2,1,0:T(8,128)}, u32[]{:S(2)}, u32[]{:S(2)}) %collective-permute-start.2) | collective-permute-done | bytes 524320 | tf_op jit(solution)/shard_map/while/body/eval_jaxpr/ppermute | solution.py:29
  59.8 1.4 add_subtract_fusion.2
  61.2 2.4 add_add_fusion.2
  63.5 2.9 %fusion.41 = f32[6,32,16,1024]{3,2,1,0:T(8,128)S(1)} fusion(f32[6,32,16,256]{3,2,1,0:T(8,128)S(1)} %get-tuple-element.187, bf16[256,1024]{1,0:T(8,128)(2,1)} %get-tuple-element.202), kind=kOutput, calls=%fused_computation.18.clone.1 | convolution fusion | flops 1611399168 | bytes 16252928 | tf_op jit(solution)/shard_map/while/body/eval_jaxpr/kbnc,cd->kbnd/dot_general | solution.py:21
  66.5 10.5 %fusion.42 = f32[2,6,32,16,256]{4,3,2,1,0:T(8,128)S(1)} fusion(f32[2,6,1024]{2,1,0:T(8,128)S(1)} %get-tuple-element.204, f32[2,6,1024]{2,1,0:T(8,128)S(1)} %get-tuple-element.203, f32[6,32,16,1024]{3,2,1,0:T(8,128)S(1)} %fusion.41, bf16[1024,256]{1,0:T(8,128)(2,1)S(1)} %copy-done.2), kind=kOutput, calls=%fused_computation.9.clone.1 | convolution fusion | flops 3290431488 | bytes 19496960 | tf_op jit(solution)/shard_map/while/body/eval_jaxpr/ekbnd,dc->ekbnc/dot_general | solution.py:23
  77.0 1.5 fusion.43
  78.6 1.3 collective-permute-start
  79.9 1.5 collective-permute-done
  81.4 0.1 fusion.44
  81.5 9.3 %collective-permute-start.1 = (f32[32,16,256]{2,1,0:T(8,128)S(1)}, f32[32,16,256]{2,1,0:T(8,128)S(1)}, u32[]{:S(2)}, u32[]{:S(2)}) collective-permute-start(f32[32,16,256]{2,1,0:T(8,128)S(1)} %fusion.44), channel_id=1, source_target_pairs={{0,2},{1,3},{2,4},{3,5},{4,6},{5,7}} | collective-permute-start | bytes 1572872 | tf_op jit(solution)/shard_map/while/body/eval_jaxpr/ppermute | solution.py:29
  90.7 11.3 %collective-permute-done.1 = f32[32,16,256]{2,1,0:T(8,128)S(1)} collective-permute-done((f32[32,16,256]{2,1,0:T(8,128)S(1)}, f32[32,16,256]{2,1,0:T(8,128)S(1)}, u32[]{:S(2)}, u32[]{:S(2)}) %collective-permute-start.1) | collective-permute-done | bytes 524320 | tf_op jit(solution)/shard_map/while/body/eval_jaxpr/ppermute | solution.py:29
  102.0 0.9 add.127
  102.9 7.2 %collective-permute-start.2 = (f32[32,16,256]{2,1,0:T(8,128)}, f32[32,16,256]{2,1,0:T(8,128)}, u32[]{:S(2)}, u32[]{:S(2)}) collective-permute-start(f32[32,16,256]{2,1,0:T(8,128)} %add.127), channel_id=1, source_target_pairs={{0,4},{1,5},{2,6},{3,7}} | collective-permute-start | bytes 1572872 | tf_op jit(solution)/shard_map/while/body/eval_jaxpr/ppermute | solution.py:29
  110.1 1.7 slice.48
  111.8 5.0 %collective-permute-done.2 = f32[32,16,256]{2,1,0:T(8,128)} collective-permute-done((f32[32,16,256]{2,1,0:T(8,128)}, f32[32,16,256]{2,1,0:T(8,128)}, u32[]{:S(2)}, u32[]{:S(2)}) %collective-permute-start.2) | collective-permute-done | bytes 524320 | tf_op jit(solution)/shard_map/while/body/eval_jaxpr/ppermute | solution.py:29
  116.8 1.4 add_subtract_fusion.2
  118.2 2.4 add_add_fusion.2
  120.6 0.0 copy-start.2
  120.6 2.9 %fusion.41 = f32[6,32,16,1024]{3,2,1,0:T(8,128)S(1)} fusion(f32[6,32,16,256]{3,2,1,0:T(8,128)S(1)} %get-tuple-element.187, bf16[256,1024]{1,0:T(8,128)(2,1)} %get-tuple-element.202), kind=kOutput, calls=%fused_computation.18.clone.1 | convolution fusion | flops 1611399168 | bytes 16252928 | tf_op jit(solution)/shard_map/while/body/eval_jaxpr/kbnc,cd->kbnd/dot_general | solution.py:21
  123.5 10.5 %fusion.42 = f32[2,6,32,16,256]{4,3,2,1,0:T(8,128)S(1)} fusion(f32[2,6,1024]{2,1,0:T(8,128)S(1)} %get-tuple-element.204, f32[2,6,1024]{2,1,0:T(8,128)S(1)} %get-tuple-element.203, f32[6,32,16,1024]{3,2,1,0:T(8,128)S(1)} %fusion.41, bf16[1024,256]{1,0:T(8,128)(2,1)S(1)} %copy-done.2), kind=kOutput, calls=%fused_computation.9.clone.1 | convolution fusion | flops 3290431488 | bytes 19496960 | tf_op jit(solution)/shard_map/while/body/eval_jaxpr/ekbnd,dc->ekbnc/dot_general | solution.py:23
  134.0 1.5 fusion.43
  135.6 1.3 collective-permute-start
  136.9 1.5 collective-permute-done
  138.4 0.1 fusion.44
  138.5 11.8 %collective-permute-start.1 = (f32[32,16,256]{2,1,0:T(8,128)S(1)}, f32[32,16,256]{2,1,0:T(8,128)S(1)}, u32[]{:S(2)}, u32[]{:S(2)}) collective-permute-start(f32[32,16,256]{2,1,0:T(8,128)S(1)} %fusion.44), channel_id=1, source_target_pairs={{0,2},{1,3},{2,4},{3,5},{4,6},{5,7}} | collective-permute-start | bytes 1572872 | tf_op jit(solution)/shard_map/while/body/eval_jaxpr/ppermute | solution.py:29
  150.3 10.6 %collective-permute-done.1 = f32[32,16,256]{2,1,0:T(8,128)S(1)} collective-permute-done((f32[32,16,256]{2,1,0:T(8,128)S(1)}, f32[32,16,256]{2,1,0:T(8,128)S(1)}, u32[]{:S(2)}, u32[]{:S(2)}) %collective-permute-start.1) | collective-permute-done | bytes 524320 | tf_op jit(solution)/shard_map/while/body/eval_jaxpr/ppermute | solution.py:29
  161.0 0.9 add.127
  161.9 7.1 %collective-permute-start.2 = (f32[32,16,256]{2,1,0:T(8,128)}, f32[32,16,256]{2,1,0:T(8,128)}, u32[]{:S(2)}, u32[]{:S(2)}) collective-permute-start(f32[32,16,256]{2,1,0:T(8,128)} %add.127), channel_id=1, source_target_pairs={{0,4},{1,5},{2,6},{3,7}} | collective-permute-start | bytes 1572872 | tf_op jit(solution)/shard_map/while/body/eval_jaxpr/ppermute | solution.py:29
  169.0 1.7 slice.48
  170.7 6.6 %collective-permute-done.2 = f32[32,16,256]{2,1,0:T(8,128)} collective-permute-done((f32[32,16,256]{2,1,0:T(8,128)}, f32[32,16,256]{2,1,0:T(8,128)}, u32[]{:S(2)}, u32[]{:S(2)}) %collective-permute-start.2) | collective-permute-done | bytes 524320 | tf_op jit(solution)/shard_map/while/body/eval_jaxpr/ppermute | solution.py:29
  177.3 1.4 add_subtract_fusion.2
  178.7 2.4 add_add_fusion.2
  181.0 0.0 copy-start.2
  181.0 2.9 %fusion.41 = f32[6,32,16,1024]{3,2,1,0:T(8,128)S(1)} fusion(f32[6,32,16,256]{3,2,1,0:T(8,128)S(1)} %get-tuple-element.187, bf16[256,1024]{1,0:T(8,128)(2,1)} %get-tuple-element.202), kind=kOutput, calls=%fused_computation.18.clone.1 | convolution fusion | flops 1611399168 | bytes 16252928 | tf_op jit(solution)/shard_map/while/body/eval_jaxpr/kbnc,cd->kbnd/dot_general | solution.py:21
  184.0 10.5 %fusion.42 = f32[2,6,32,16,256]{4,3,2,1,0:T(8,128)S(1)} fusion(f32[2,6,1024]{2,1,0:T(8,128)S(1)} %get-tuple-element.204, f32[2,6,1024]{2,1,0:T(8,128)S(1)} %get-tuple-element.203, f32[6,32,16,1024]{3,2,1,0:T(8,128)S(1)} %fusion.41, bf16[1024,256]{1,0:T(8,128)(2,1)S(1)} %copy-done.2), kind=kOutput, calls=%fused_computation.9.clone.1 | convolution fusion | flops 3290431488 | bytes 19496960 | tf_op jit(solution)/shard_map/while/body/eval_jaxpr/ekbnd,dc->ekbnc/dot_general | solution.py:23
  194.5 1.5 fusion.43
  196.1 1.3 collective-permute-start
  197.4 1.5 collective-permute-done
  198.9 0.1 fusion.44
  199.0 8.1 %collective-permute-start.1 = (f32[32,16,256]{2,1,0:T(8,128)S(1)}, f32[32,16,256]{2,1,0:T(8,128)S(1)}, u32[]{:S(2)}, u32[]{:S(2)}) collective-permute-start(f32[32,16,256]{2,1,0:T(8,128)S(1)} %fusion.44), channel_id=1, source_target_pairs={{0,2},{1,3},{2,4},{3,5},{4,6},{5,7}} | collective-permute-start | bytes 1572872 | tf_op jit(solution)/shard_map/while/body/eval_jaxpr/ppermute | solution.py:29
  207.1 10.1 %collective-permute-done.1 = f32[32,16,256]{2,1,0:T(8,128)S(1)} collective-permute-done((f32[32,16,256]{2,1,0:T(8,128)S(1)}, f32[32,16,256]{2,1,0:T(8,128)S(1)}, u32[]{:S(2)}, u32[]{:S(2)}) %collective-permute-start.1) | collective-permute-done | bytes 524320 | tf_op jit(solution)/shard_map/while/body/eval_jaxpr/ppermute | solution.py:29
  217.2 0.9 add.127
  218.1 9.5 %collective-permute-start.2 = (f32[32,16,256]{2,1,0:T(8,128)}, f32[32,16,256]{2,1,0:T(8,128)}, u32[]{:S(2)}, u32[]{:S(2)}) collective-permute-start(f32[32,16,256]{2,1,0:T(8,128)} %add.127), channel_id=1, source_target_pairs={{0,4},{1,5},{2,6},{3,7}} | collective-permute-start | bytes 1572872 | tf_op jit(solution)/shard_map/while/body/eval_jaxpr/ppermute | solution.py:29
  227.6 1.7 slice.48
  229.3 4.6 %collective-permute-done.2 = f32[32,16,256]{2,1,0:T(8,128)} collective-permute-done((f32[32,16,256]{2,1,0:T(8,128)}, f32[32,16,256]{2,1,0:T(8,128)}, u32[]{:S(2)}, u32[]{:S(2)}) %collective-permute-start.2) | collective-permute-done | bytes 524320 | tf_op jit(solution)/shard_map/while/body/eval_jaxpr/ppermute | solution.py:29
  233.9 1.4 add_subtract_fusion.2
  235.3 2.4 add_add_fusion.2
  237.7 1.7 copy-done
  (12 shorter events, 0.2 us)
Async XLA Ops:
  0.0 3.6 %copy-start.1 = (f32[6]{0:T(128)S(1)}, f32[6]{0:T(128)}, u32[]{:S(2)}) copy-start(f32[6]{0:T(128)} %param.18) | copy-start | bytes 76
  3.6 2.9 %copy-start.2 = (bf16[1024,256]{1,0:T(8,128)(2,1)S(1)}, bf16[1024,256]{1,0:T(8,128)(2,1)}, u32[]{:S(2)}) copy-start(bf16[1024,256]{1,0:T(8,128)(2,1)} %get-tuple-element.205) | copy-start | bytes 1572868 | tf_op jit(solution)/shard_map/while
  18.7 4.3 %collective-permute-start = (f32[32,16,256]{2,1,0:T(8,128)S(1)}, f32[32,16,256]{2,1,0:T(8,128)S(1)}, u32[]{:S(2)}, u32[]{:S(2)}) collective-permute-start(f32[32,16,256]{2,1,0:T(8,128)S(1)} %slice_bitcast_fusion.2), channel_id=1, source_target_pairs={{0,1},{1,2},{2,3},{3,4},{4,5},{5,6},{6,7}} | collective-permute-start | bytes 1572872 | tf_op jit(solution)/shard_map/while/body/eval_jaxpr/ppermute | solution.py:29
  23.0 21.9 %collective-permute-start.1 = (f32[32,16,256]{2,1,0:T(8,128)S(1)}, f32[32,16,256]{2,1,0:T(8,128)S(1)}, u32[]{:S(2)}, u32[]{:S(2)}) collective-permute-start(f32[32,16,256]{2,1,0:T(8,128)S(1)} %fusion.44), channel_id=1, source_target_pairs={{0,2},{1,3},{2,4},{3,5},{4,6},{5,7}} | collective-permute-start | bytes 1572872 | tf_op jit(solution)/shard_map/while/body/eval_jaxpr/ppermute | solution.py:29
  45.8 14.0 %collective-permute-start.2 = (f32[32,16,256]{2,1,0:T(8,128)}, f32[32,16,256]{2,1,0:T(8,128)}, u32[]{:S(2)}, u32[]{:S(2)}) collective-permute-start(f32[32,16,256]{2,1,0:T(8,128)} %add.127), channel_id=1, source_target_pairs={{0,4},{1,5},{2,6},{3,7}} | collective-permute-start | bytes 1572872 | tf_op jit(solution)/shard_map/while/body/eval_jaxpr/ppermute | solution.py:29
  63.5 2.9 %copy-start.2 = (bf16[1024,256]{1,0:T(8,128)(2,1)S(1)}, bf16[1024,256]{1,0:T(8,128)(2,1)}, u32[]{:S(2)}) copy-start(bf16[1024,256]{1,0:T(8,128)(2,1)} %get-tuple-element.205) | copy-start | bytes 1572868 | tf_op jit(solution)/shard_map/while
  78.6 2.8 %collective-permute-start = (f32[32,16,256]{2,1,0:T(8,128)S(1)}, f32[32,16,256]{2,1,0:T(8,128)S(1)}, u32[]{:S(2)}, u32[]{:S(2)}) collective-permute-start(f32[32,16,256]{2,1,0:T(8,128)S(1)} %slice_bitcast_fusion.2), channel_id=1, source_target_pairs={{0,1},{1,2},{2,3},{3,4},{4,5},{5,6},{6,7}} | collective-permute-start | bytes 1572872 | tf_op jit(solution)/shard_map/while/body/eval_jaxpr/ppermute | solution.py:29
  81.5 20.5 %collective-permute-start.1 = (f32[32,16,256]{2,1,0:T(8,128)S(1)}, f32[32,16,256]{2,1,0:T(8,128)S(1)}, u32[]{:S(2)}, u32[]{:S(2)}) collective-permute-start(f32[32,16,256]{2,1,0:T(8,128)S(1)} %fusion.44), channel_id=1, source_target_pairs={{0,2},{1,3},{2,4},{3,5},{4,6},{5,7}} | collective-permute-start | bytes 1572872 | tf_op jit(solution)/shard_map/while/body/eval_jaxpr/ppermute | solution.py:29
  102.9 14.0 %collective-permute-start.2 = (f32[32,16,256]{2,1,0:T(8,128)}, f32[32,16,256]{2,1,0:T(8,128)}, u32[]{:S(2)}, u32[]{:S(2)}) collective-permute-start(f32[32,16,256]{2,1,0:T(8,128)} %add.127), channel_id=1, source_target_pairs={{0,4},{1,5},{2,6},{3,7}} | collective-permute-start | bytes 1572872 | tf_op jit(solution)/shard_map/while/body/eval_jaxpr/ppermute | solution.py:29
  120.6 2.9 %copy-start.2 = (bf16[1024,256]{1,0:T(8,128)(2,1)S(1)}, bf16[1024,256]{1,0:T(8,128)(2,1)}, u32[]{:S(2)}) copy-start(bf16[1024,256]{1,0:T(8,128)(2,1)} %get-tuple-element.205) | copy-start | bytes 1572868 | tf_op jit(solution)/shard_map/while
  135.6 2.8 %collective-permute-start = (f32[32,16,256]{2,1,0:T(8,128)S(1)}, f32[32,16,256]{2,1,0:T(8,128)S(1)}, u32[]{:S(2)}, u32[]{:S(2)}) collective-permute-start(f32[32,16,256]{2,1,0:T(8,128)S(1)} %slice_bitcast_fusion.2), channel_id=1, source_target_pairs={{0,1},{1,2},{2,3},{3,4},{4,5},{5,6},{6,7}} | collective-permute-start | bytes 1572872 | tf_op jit(solution)/shard_map/while/body/eval_jaxpr/ppermute | solution.py:29
  138.5 22.5 %collective-permute-start.1 = (f32[32,16,256]{2,1,0:T(8,128)S(1)}, f32[32,16,256]{2,1,0:T(8,128)S(1)}, u32[]{:S(2)}, u32[]{:S(2)}) collective-permute-start(f32[32,16,256]{2,1,0:T(8,128)S(1)} %fusion.44), channel_id=1, source_target_pairs={{0,2},{1,3},{2,4},{3,5},{4,6},{5,7}} | collective-permute-start | bytes 1572872 | tf_op jit(solution)/shard_map/while/body/eval_jaxpr/ppermute | solution.py:29
  161.9 15.4 %collective-permute-start.2 = (f32[32,16,256]{2,1,0:T(8,128)}, f32[32,16,256]{2,1,0:T(8,128)}, u32[]{:S(2)}, u32[]{:S(2)}) collective-permute-start(f32[32,16,256]{2,1,0:T(8,128)} %add.127), channel_id=1, source_target_pairs={{0,4},{1,5},{2,6},{3,7}} | collective-permute-start | bytes 1572872 | tf_op jit(solution)/shard_map/while/body/eval_jaxpr/ppermute | solution.py:29
  181.0 2.9 %copy-start.2 = (bf16[1024,256]{1,0:T(8,128)(2,1)S(1)}, bf16[1024,256]{1,0:T(8,128)(2,1)}, u32[]{:S(2)}) copy-start(bf16[1024,256]{1,0:T(8,128)(2,1)} %get-tuple-element.205) | copy-start | bytes 1572868 | tf_op jit(solution)/shard_map/while
  196.1 2.8 %collective-permute-start = (f32[32,16,256]{2,1,0:T(8,128)S(1)}, f32[32,16,256]{2,1,0:T(8,128)S(1)}, u32[]{:S(2)}, u32[]{:S(2)}) collective-permute-start(f32[32,16,256]{2,1,0:T(8,128)S(1)} %slice_bitcast_fusion.2), channel_id=1, source_target_pairs={{0,1},{1,2},{2,3},{3,4},{4,5},{5,6},{6,7}} | collective-permute-start | bytes 1572872 | tf_op jit(solution)/shard_map/while/body/eval_jaxpr/ppermute | solution.py:29
  199.0 18.2 %collective-permute-start.1 = (f32[32,16,256]{2,1,0:T(8,128)S(1)}, f32[32,16,256]{2,1,0:T(8,128)S(1)}, u32[]{:S(2)}, u32[]{:S(2)}) collective-permute-start(f32[32,16,256]{2,1,0:T(8,128)S(1)} %fusion.44), channel_id=1, source_target_pairs={{0,2},{1,3},{2,4},{3,5},{4,6},{5,7}} | collective-permute-start | bytes 1572872 | tf_op jit(solution)/shard_map/while/body/eval_jaxpr/ppermute | solution.py:29
  218.1 15.9 %collective-permute-start.2 = (f32[32,16,256]{2,1,0:T(8,128)}, f32[32,16,256]{2,1,0:T(8,128)}, u32[]{:S(2)}, u32[]{:S(2)}) collective-permute-start(f32[32,16,256]{2,1,0:T(8,128)} %add.127), channel_id=1, source_target_pairs={{0,4},{1,5},{2,6},{3,7}} | collective-permute-start | bytes 1572872 | tf_op jit(solution)/shard_map/while/body/eval_jaxpr/ppermute | solution.py:29
  237.7 1.7 copy-start
where the time goes:
time: 240 us; the launch traced here: 239 us
  starting transfers between devices  77.8 us (32%)
  waiting for transfers between devices  70.4 us (29%)
  matrix products  53.6 us (22%)
  other arithmetic  26.4 us (11%)
  local copies, waits for them, and re-layouts  10.2 us (4%)
    ppermute x12, starting transfers between devices, sweep(): prefix = prefix + lax.ppermute(prefix, 'time', perm)  77.8 us
    ppermute x12, waiting for transfers between devices, sweep(): prefix = prefix + lax.ppermute(prefix, 'time', perm)  70.4 us
    dot_general x4, matrix products, sweep(): jnp.einsum('ekbnd,dc->ekbnc', act, w_out, preferred_element_type=jnp.floa...  42 us
    dot_general x4, matrix products, sweep(): jnp.einsum('kbnc,cd->kbnd', states.astype(jnp.bfloat16), w_in, preferred_...  11.6 us
    add x4, other arithmetic, sweep(): return x_init[None] + (before[None] + local_before)  9.43 us
    slice x4, local copies, waits for them, and re-layouts, sweep(): running[:-1]  6.92 us
    another operation x4, other arithmetic, sweep(): running = jnp.cumsum(drift, axis=0)  6.17 us
    sub x4, other arithmetic, sweep(): before = prefix - dev_total  5.47 us
  transfers between devices with their start and end apart: 12, of which 12 were waited for; matrix products, arithmetic and copies ran while one was open for 3% of the time, Pallas kernels for 0%

commit v1 on v0

v1 whole, which is shorter than its diff:
```python
import functools
import math

import jax
import jax.numpy as jnp
from jax import lax
from jax.experimental import pallas as pl
from jax.experimental.pallas import tpu as pltpu
from jax.sharding import PartitionSpec as P

NUM_SWEEPS = 4
ROOT = math.sqrt(2.0 / math.pi)
LIN = 2.0 * ROOT
CUB = 8.0 * ROOT * 0.044715
CH = 32
DUO = 2
NCH = 4
NB = NUM_SWEEPS * NCH
OWN = CH * DUO * NCH
STEPS = 6
PAIR = 2 * STEPS
ROWS = PAIR * CH
WIDTH = 256
HIDDEN = 1024
NEED = 3
MESH = pl.DeviceIdType.MESH

dot = functools.partial(jnp.dot, preferred_element_type=jnp.float32)


def half_gelu(pre, gain, shift):
    half = pre * gain + shift
    arg = half * (half * half * CUB + LIN)
    return (half * (1.0 + jnp.tanh(arg))).astype(jnp.bfloat16)


def kernel(x_ref, w_in, w_out, gamma_c, beta_c, gamma_u, beta_u, h_ref, guide_ref, loc_out, base_out, loc, base, par, hvec, sib_par, w1, xb, abuf,
           tbuf, vbuf, rec, sib_send, sib_recv, send_sem, recv_sem, out_send, out_recv):
    time = lax.axis_index("time")
    data = lax.axis_index("data")
    core = lax.rem(time, 2)
    chip = lax.div(time, 2)
    sibling = time + 1 - 2 * core
    row0 = pl.multiple_of(core * OWN, OWN)

    def peer(step):
        return lax.rem(time + 2 * step, 8)

    barrier = pltpu.get_barrier_semaphore()
    for other in (sibling, peer(1), peer(2), peer(3)):
        pl.semaphore_signal(barrier, inc=1, device_id=(data, other), device_id_type=MESH)
    pl.semaphore_wait(barrier, 4)

    def remote(src, dst, send, recv, target):
        return pltpu.make_async_remote_copy(src_ref=src, dst_ref=dst, send_sem=send, recv_sem=recv, device_id=(data, target), device_id_type=MESH)

    own = pl.ds(core * STEPS, STEPS)
    for k in range(STEPS):
        hvec[core * STEPS + k] = jnp.full((8, 128), h_ref[k], jnp.float32)
    raw = [gamma_c, beta_c, gamma_u, beta_u]
    par_copies = [remote(raw[i], sib_par.at[i], sib_send.at[i], sib_recv.at[i], sibling) for i in range(4)]
    par_copies.append(remote(hvec.at[own], hvec.at[own], sib_send.at[4], sib_recv.at[4], sibling))
    for copy in par_copies:
        copy.start()

    def spread(refs, first):
        for i in range(4):
            full = refs[i][...].astype(jnp.float32)
            full = 0.5 * (1.0 + full) if i % 2 == 0 else 0.5 * full
            for k in range(STEPS):
                par[first + k, i] = jnp.broadcast_to(full[k:k + 1], (8, HIDDEN))

    def round_rows(c):
        return pl.ds(pl.multiple_of(row0 + c * (DUO * CH), DUO * CH), DUO * CH)

    spread(raw, core * STEPS)
    for n in range(4):
        w1[n] = w_in[:, 256 * n:256 * n + 256]
    loc[...] = jnp.zeros_like(loc)
    for c in range(NCH):
        base[c] = x_ref[round_rows(c), :].reshape(DUO, CH, WIDTH)
    for copy in par_copies:
        copy.wait()
    spread([sib_par.at[i] for i in range(4)], (1 - core) * STEPS)

    guide = guide_ref[0]

    def stage_x(i, c):
        for t in range(PAIR):
            value = base[c, i] if t == 0 else base[c, i] + loc[t, c, i]
            xb[i, CH * t:CH * t + CH, :] = value.astype(jnp.bfloat16)

    def stage_a(i):
        for n in range(4):
            abuf[i, n] = dot(xb[i], w1[n])

    def gelus(i, n):
        lanes = slice(256 * n, 256 * n + 256)
        cond, free = [], []
        for t in range(PAIR):
            wide = [jnp.concatenate([par[t, p, :, lanes]] * (CH // 8), axis=0) for p in range(4)]
            pre = abuf[i, n, CH * t:CH * t + CH, :]
            cond.append(half_gelu(pre, wide[0], wide[1]))
            free.append(half_gelu(pre, wide[2], wide[3]))
        return jnp.concatenate(cond, axis=0), jnp.concatenate(free, axis=0)

    def stage_f(i, c, event, f_c, f_u):
        total = None
        for t in range(PAIR):
            rows = slice(CH * t, CH * t + CH)
            hk = jnp.concatenate([jnp.concatenate([hvec[t]] * 2, axis=1)] * (CH // 8), axis=0)
            drift = hk * ((1.0 + guide) * f_c[rows] - guide * f_u[rows])
            total = drift if total is None else total + drift
            if t + 1 < PAIR:
                loc[t + 1, c, i] = total
            else:
                tbuf[event, i] = total

    def copy_to(lane, e, src, step):
        return remote(src, rec.at[lane, e], send_sem.at[step - 1, e], recv_sem.at[lane, e], peer(step))

    def send_sum(e):
        @pl.when(chip == 0)
        def _():
            copy_to(0, e, tbuf.at[e], 1).start()

        @pl.when(chip == 2)
        def _():
            copy_to(1, e, tbuf.at[e], 1).start()

    def got(lane, e):
        remote(rec.at[lane, e], rec.at[lane, e], send_sem.at[0, e], recv_sem.at[lane, e], peer(1)).wait_recv()

    def set_base(e, total, last):
        c = lax.rem(e, NCH)
        rows = round_rows(c)
        value = x_ref[rows, :].reshape(DUO, CH, WIDTH)
        if total is not None:
            value = value + total
        if last:
            base_out[rows, :] = value.reshape(DUO * CH, WIDTH)
            remote(base_out.at[rows], base_out.at[rows], out_send.at[1, c], out_recv.at[1, c], sibling).start()
        else:
            base[c] = value

    def take(e, last):
        @pl.when(chip == 1)
        def _():
            got(0, e)
            below = rec[0, e]
            vbuf[e] = below + tbuf[e]
            copy_to(0, e, vbuf.at[e], 1).start()
            copy_to(0, e, vbuf.at[e], 2).start()
            set_base(e, below, last)

        @pl.when(chip == 2)
        def _():
            got(0, e)
            set_base(e, rec[0, e], last)

        @pl.when(chip == 3)
        def _():
            got(0, e)
            got(1, e)
            set_base(e, rec[0, e] + rec[1, e], last)

    def send_local(e):
        c = lax.rem(e, NCH)
        for k in range(STEPS):
            loc_out[k, core * NCH + c] = loc[core * STEPS + k, c]
        local_copy(c).start()

    def local_copy(c):
        return remote(loc.at[pl.ds((1 - core) * STEPS, STEPS), c], loc_out.at[:, core * NCH + c], out_send.at[0, c], out_recv.at[0, c], sibling)

    def one_round(r, carry):
        c = lax.rem(r, NCH)
        c_next = lax.rem(r + 1, NCH)

        @pl.when(r >= 1)
        def _():
            send_sum(r - 1)

        @pl.when((r >= NEED) & (r < NEED + NB - NCH))
        def _():
            take(r - NEED, False)

        @pl.when(r >= NEED + NB - NCH)
        def _():
            take(r - NEED, True)

        @pl.when(r >= NB - NCH + 1)
        def _():
            send_local(r - 1)

        for i in range(DUO):
            follow = (i + 1) % DUO
            stage_x(follow, c if i + 1 < DUO else c_next)
            f_c = f_u = None
            for n in range(4):
                weight = w_out[256 * n:256 * n + 256, :]
                cond, free = gelus(i, n)
                part_c, part_u = dot(cond, weight), dot(free, weight)
                f_c = part_c if n == 0 else f_c + part_c
                f_u = part_u if n == 0 else f_u + part_u
                if n == 1:
                    stage_a(follow)
            stage_f(i, c, r, f_c, f_u)
        return carry

    stage_x(0, 0)
    stage_a(0)
    lax.fori_loop(0, NB, one_round, 0)
    send_sum(NB - 1)
    send_local(NB - 1)

    @pl.when(chip == 0)
    def _():
        for c in range(NCH):
            set_base(c, None, True)

    for e in range(NB - NEED, NB):
        take(e, True)

    def drain(e, carry):
        @pl.when((chip == 0) | (chip == 2))
        def _():
            copy_to(0, e, tbuf.at[e], 1).wait_send()

        @pl.when(chip == 1)
        def _():
            copy_to(0, e, vbuf.at[e], 1).wait_send()
            copy_to(0, e, vbuf.at[e], 2).wait_send()
        return carry

    def finish_out(c, carry):
        rows = round_rows(c)
        local_copy(c).wait()
        remote(base_out.at[rows], base_out.at[rows], out_send.at[1, c], out_recv.at[1, c], sibling).wait()
        return carry

    lax.fori_loop(0, NB, drain, 0)
    lax.fori_loop(0, NCH, finish_out, 0)


def solution(mesh):
    vmem = pl.BlockSpec(memory_space=pltpu.VMEM)
    smem = pl.BlockSpec(memory_space=pltpu.SMEM)
    dma = pltpu.SemaphoreType.DMA

    def local(x_init, w_in, w_out, gamma_c, beta_c, gamma_u, beta_u, step_h, guide_w):
        samples, tokens, width = x_init.shape
        rows = samples * tokens
        loc, base = pl.pallas_call(
            kernel,
            out_shape=(jax.ShapeDtypeStruct((STEPS, 2 * NCH, DUO, CH, width), jnp.float32), jax.ShapeDtypeStruct((rows, width), jnp.float32)),
            in_specs=[vmem] * 7 + [smem] * 2,
            out_specs=(vmem, vmem),
            scratch_shapes=[
                pltpu.VMEM((PAIR, NCH, DUO, CH, WIDTH), jnp.float32),
                pltpu.VMEM((NCH, DUO, CH, WIDTH), jnp.float32),
                pltpu.VMEM((PAIR, 4, 8, HIDDEN), jnp.float32),
                pltpu.VMEM((PAIR, 8, 128), jnp.float32),
                pltpu.VMEM((4, STEPS, HIDDEN), jnp.bfloat16),
                pltpu.VMEM((4, WIDTH, WIDTH), jnp.bfloat16),
                pltpu.VMEM((DUO, ROWS, WIDTH), jnp.bfloat16),
                pltpu.VMEM((DUO, 4, ROWS, WIDTH), jnp.float32),
                pltpu.VMEM((NB, DUO, CH, WIDTH), jnp.float32),
                pltpu.VMEM((NB, DUO, CH, WIDTH), jnp.float32),
                pltpu.VMEM((2, NB, DUO, CH, WIDTH), jnp.float32),
                dma((5,)), dma((5,)), dma((2, NB)), dma((2, NB)), dma((2, NCH)), dma((2, NCH)),
            ],
            compiler_params=pltpu.CompilerParams(collective_id=0, has_side_effects=True, vmem_limit_bytes=48 * 2 ** 20),
            name="picard",
        )(x_init.reshape(rows, width), w_in, w_out, gamma_c, beta_c, gamma_u, beta_u, step_h, guide_w)
        return (base[None] + loc.reshape(STEPS, rows, width)).reshape(STEPS, samples, tokens, width)

    return jax.shard_map(local, mesh=mesh, in_specs=(P("data", None, None), P(None, None), P(None, None), P("time", None), P("time", None), P("time", None), P("time", None), P("time"), P(None)), out_specs=P("time", "data", None, None), check_vma=False)
```

time: 240 us -> 61.7 us (0.26)
  the two profiles are of different devices: /device:TPU:0 before, /device:TPU:5 now
where the time goes in v1:
time: 61.7 us; the launch traced here: 61.2 us
  Pallas kernels  51.8 us (84%)
  local copies, waits for them, and re-layouts  6.64 us (11%)
  other arithmetic  2.09 us (3%)
  between operations  0.68 us (1%)
    pallas_call x1, Pallas kernels, local(): pl.pallas_call(kernel, out_shape=(jax.ShapeDtypeStruct((STEPS, 2 * NCH, D...  51.8 us
    unnamed x16, local copies, waits for them, and re-layouts  6.64 us
    add x1, other arithmetic, local(): base[None] + loc.reshape(STEPS, rows, width)  2.09 us

profile of v1, /device:TPU:5, one launch (start us, length us, event | category | flops | bytes accessed | tf_op | source)
XLA Modules:
  0.0 61.2 jit_solution(1476082675270484033)
XLA Ops:
  0.7 0.0 copy-start
  0.7 1.0 %copy-done = f32[32,16,256]{2,1,0:T(8,128)S(1)} copy-done((f32[32,16,256]{2,1,0:T(8,128)S(1)}, f32[32,16,256]{2,1,0:T(8,128)}, u32[]{:S(2)}) %copy-start) | copy-done | bytes 524312
  1.7 0.0 copy-start.1
  1.7 1.0 %copy-done.1 = bf16[256,1024]{1,0:T(8,128)(2,1)S(1)} copy-done((bf16[256,1024]{1,0:T(8,128)(2,1)S(1)}, bf16[256,1024]{1,0:T(8,128)(2,1)}, u32[]{:S(2)}) %copy-start.1) | copy-done | bytes 524312
  2.7 0.0 copy-start.2
  2.7 1.0 %copy-done.2 = bf16[1024,256]{1,0:T(8,128)(2,1)S(1)} copy-done((bf16[1024,256]{1,0:T(8,128)(2,1)S(1)}, bf16[1024,256]{1,0:T(8,128)(2,1)}, u32[]{:S(2)}) %copy-start.2) | copy-done | bytes 524312
  3.8 0.0 copy-start.3
  3.8 0.7 %copy-done.3 = bf16[6,1024]{1,0:T(8,128)(2,1)S(1)} copy-done((bf16[6,1024]{1,0:T(8,128)(2,1)S(1)}, bf16[6,1024]{1,0:T(8,128)(2,1)}, u32[]{:S(2)}) %copy-start.3) | copy-done | bytes 12312
  4.5 0.0 copy-start.4
  4.5 0.7 %copy-done.4 = bf16[6,1024]{1,0:T(8,128)(2,1)S(1)} copy-done((bf16[6,1024]{1,0:T(8,128)(2,1)S(1)}, bf16[6,1024]{1,0:T(8,128)(2,1)}, u32[]{:S(2)}) %copy-start.4) | copy-done | bytes 12312
  5.2 0.0 copy-start.5
  5.2 0.7 %copy-done.5 = bf16[6,1024]{1,0:T(8,128)(2,1)S(1)} copy-done((bf16[6,1024]{1,0:T(8,128)(2,1)S(1)}, bf16[6,1024]{1,0:T(8,128)(2,1)}, u32[]{:S(2)}) %copy-start.5) | copy-done | bytes 12312
  5.9 0.0 copy-start.6
  5.9 0.7 %copy-done.6 = bf16[6,1024]{1,0:T(8,128)(2,1)S(1)} copy-done((bf16[6,1024]{1,0:T(8,128)(2,1)S(1)}, bf16[6,1024]{1,0:T(8,128)(2,1)}, u32[]{:S(2)}) %copy-start.6) | copy-done | bytes 12312
  6.7 0.0 copy-start.7
  6.7 0.7 %copy-done.7 = f32[6]{0:T(128)S(1)} copy-done((f32[6]{0:T(128)S(1)}, f32[6]{0:T(128)}, u32[]{:S(2)}) %copy-start.7) | copy-done | bytes 48
  7.3 51.8 %picard.1 = (f32[6,8,2,32,256]{4,3,2,1,0:T(8,128)S(1)}, f32[512,256]{1,0:T(8,128)S(1)}) custom-call(f32[512,256]{1,0:T(8,128)S(1)} %bitcast.4, bf16[256,1024]{1,0:T(8,128)(2,1)S(1)} %copy-done.1, bf16[1024,256]{1,0:T(8,128)(2,1)S(1)} %copy-done.2, bf16[6,1024]{1,0:T(8,128)(2,1)S(1)} %copy-done.3, bf16[6,1024]{1,0:T(8,128)(2,1)S(1)} %copy-done.4, ...), custom_call_target="tpu_custom_call" | custom-call | tf_op jit(solution)/shard_map/picard/pallas_call | solution.py:254
  59.1 2.1 %broadcast_add_fusion = f32[6,32,16,256]{3,2,1,0:T(8,128)} fusion(f32[6,32,16,256]{3,2,1,0:T(8,128)S(1)} %bitcast.3, f32[32,16,256]{2,1,0:T(8,128)S(1)} %bitcast.5), kind=kLoop, calls=%fused_computation | loop fusion | flops 786432 | bytes 6815744 | tf_op jit(solution)/shard_map/add | solution.py:276
Async XLA Ops:
  0.7 1.0 %copy-start = (f32[32,16,256]{2,1,0:T(8,128)S(1)}, f32[32,16,256]{2,1,0:T(8,128)}, u32[]{:S(2)}) copy-start(f32[32,16,256]{2,1,0:T(8,128)} %param.9) | copy-start | bytes 1572868
  1.7 1.0 %copy-start.1 = (bf16[256,1024]{1,0:T(8,128)(2,1)S(1)}, bf16[256,1024]{1,0:T(8,128)(2,1)}, u32[]{:S(2)}) copy-start(bf16[256,1024]{1,0:T(8,128)(2,1)} %w_in.1) | copy-start | bytes 1572868
  2.7 1.0 %copy-start.2 = (bf16[1024,256]{1,0:T(8,128)(2,1)S(1)}, bf16[1024,256]{1,0:T(8,128)(2,1)}, u32[]{:S(2)}) copy-start(bf16[1024,256]{1,0:T(8,128)(2,1)} %w_out.1) | copy-start | bytes 1572868
  3.8 0.7 %copy-start.3 = (bf16[6,1024]{1,0:T(8,128)(2,1)S(1)}, bf16[6,1024]{1,0:T(8,128)(2,1)}, u32[]{:S(2)}) copy-start(bf16[6,1024]{1,0:T(8,128)(2,1)} %gamma_c.1) | copy-start | bytes 36868
  4.5 0.7 %copy-start.4 = (bf16[6,1024]{1,0:T(8,128)(2,1)S(1)}, bf16[6,1024]{1,0:T(8,128)(2,1)}, u32[]{:S(2)}) copy-start(bf16[6,1024]{1,0:T(8,128)(2,1)} %beta_c.1) | copy-start | bytes 36868
  5.2 0.7 %copy-start.5 = (bf16[6,1024]{1,0:T(8,128)(2,1)S(1)}, bf16[6,1024]{1,0:T(8,128)(2,1)}, u32[]{:S(2)}) copy-start(bf16[6,1024]{1,0:T(8,128)(2,1)} %gamma_u.1) | copy-start | bytes 36868
  5.9 0.7 %copy-start.6 = (bf16[6,1024]{1,0:T(8,128)(2,1)S(1)}, bf16[6,1024]{1,0:T(8,128)(2,1)}, u32[]{:S(2)}) copy-start(bf16[6,1024]{1,0:T(8,128)(2,1)} %beta_u.1) | copy-start | bytes 36868
  6.7 0.7 %copy-start.7 = (f32[6]{0:T(128)S(1)}, f32[6]{0:T(128)}, u32[]{:S(2)}) copy-start(f32[6]{0:T(128)} %h_ref.1) | copy-start | bytes 76

commit v2 on v1

--- a/solution.py
+++ b/solution.py
@@ -23,6 +23,7 @@
 WIDTH = 256
 HIDDEN = 1024
 NEED = 3
+PASS = 2
 MESH = pl.DeviceIdType.MESH
 
 dot = functools.partial(jnp.dot, preferred_element_type=jnp.float32)
@@ -34,8 +35,9 @@
     return (half * (1.0 + jnp.tanh(arg))).astype(jnp.bfloat16)
 
 
-def kernel(x_ref, w_in, w_out, gamma_c, beta_c, gamma_u, beta_u, h_ref, guide_ref, loc_out, base_out, loc, base, par, hvec, sib_par, w1, xb, abuf,
-           tbuf, vbuf, rec, sib_send, sib_recv, send_sem, recv_sem, out_send, out_recv):
+def kernel(x_hbm, w_in, w_out_hbm, gamma_c, beta_c, gamma_u, beta_u, h_ref, guide_ref, loc_out, base_out, x_own, w_out, loc, base, par, hvec, own_par,
+           sib_par, w1, xb, abuf, tbuf, vbuf, rec, rec_last, in_sem, sib_send, sib_recv, send_sem, recv_sem, out_send, out_recv, last_send, last_recv,
+           base_send, base_recv):
     time = lax.axis_index("time")
     data = lax.axis_index("data")
     core = lax.rem(time, 2)
@@ -46,6 +48,13 @@
     def peer(step):
         return lax.rem(time + 2 * step, 8)
 
+    raw = [gamma_c, beta_c, gamma_u, beta_u]
+    pairs = [(raw[i], own_par.at[i]) for i in range(4)] + [(x_hbm.at[core], x_own)]
+    pairs += [(w_in.at[:, pl.ds(256 * n, 256)], w1.at[n]) for n in range(4)] + [(w_out_hbm, w_out)]
+    fetches = [pltpu.make_async_copy(src, dst, in_sem.at[i]) for i, (src, dst) in enumerate(pairs)]
+    for fetch in fetches:
+        fetch.start()
+
     barrier = pltpu.get_barrier_semaphore()
     for other in (sibling, peer(1), peer(2), peer(3)):
         pl.semaphore_signal(barrier, inc=1, device_id=(data, other), device_id_type=MESH)
@@ -57,8 +66,9 @@
     own = pl.ds(core * STEPS, STEPS)
     for k in range(STEPS):
         hvec[core * STEPS + k] = jnp.full((8, 128), h_ref[k], jnp.float32)
-    raw = [gamma_c, beta_c, gamma_u, beta_u]
-    par_copies = [remote(raw[i], sib_par.at[i], sib_send.at[i], sib_recv.at[i], sibling) for i in range(4)]
+    for fetch in fetches[:4]:
+        fetch.wait()
+    par_copies = [remote(own_par.at[i], sib_par.at[i], sib_send.at[i], sib_recv.at[i], sibling) for i in range(4)]
     par_copies.append(remote(hvec.at[own], hvec.at[own], sib_send.at[4], sib_recv.at[4], sibling))
     for copy in par_copies:
         copy.start()
@@ -73,18 +83,6 @@
     def round_rows(c):
         return pl.ds(pl.multiple_of(row0 + c * (DUO * CH), DUO * CH), DUO * CH)
 
-    spread(raw, core * STEPS)
-    for n in range(4):
-        w1[n] = w_in[:, 256 * n:256 * n + 256]
-    loc[...] = jnp.zeros_like(loc)
-    for c in range(NCH):
-        base[c] = x_ref[round_rows(c), :].reshape(DUO, CH, WIDTH)
-    for copy in par_copies:
-        copy.wait()
-    spread([sib_par.at[i] for i in range(4)], (1 - core) * STEPS)
-
-    guide = guide_ref[0]
-
     def stage_x(i, c):
         for t in range(PAIR):
             value = base[c, i] if t == 0 else base[c, i] + loc[t, c, i]
@@ -93,6 +91,19 @@
     def stage_a(i):
         for n in range(4):
             abuf[i, n] = dot(xb[i], w1[n])
+
+    loc[...] = jnp.zeros_like(loc)
+    spread([own_par.at[i] for i in range(4)], core * STEPS)
+    for fetch in fetches[4:]:
+        fetch.wait()
+    base[...] = x_own[...]
+    stage_x(0, 0)
+    stage_a(0)
+    for copy in par_copies:
+        copy.wait()
+    spread([sib_par.at[i] for i in range(4)], (1 - core) * STEPS)
+
+    guide = guide_ref[0]
 
     def gelus(i, n):
         lanes = slice(256 * n, 256 * n + 256)
@@ -134,7 +145,7 @@
     def set_base(e, total, last):
         c = lax.rem(e, NCH)
         rows = round_rows(c)
-        value = x_ref[rows, :].reshape(DUO, CH, WIDTH)
+        value = x_own[c]
         if total is not None:
             value = value + total
         if last:
@@ -143,7 +154,7 @@
         else:
             base[c] = value
 
-    def take(e, last):
+    def relay(e, last):
         @pl.when(chip == 1)
         def _():
             got(0, e)
@@ -153,6 +164,7 @@
             copy_to(0, e, vbuf.at[e], 2).start()
             set_base(e, below, last)
 
+    def take(e, last):
         @pl.when(chip == 2)
         def _():
             got(0, e)
@@ -163,6 +175,33 @@
             got(0, e)
             got(1, e)
             set_base(e, rec[0, e] + rec[1, e], last)
+
+    def last_copy(source, i, step):
+        return remote(tbuf.at[NB - 1, i], rec_last.at[source, i], last_send.at[step - 1, i], last_recv.at[source, i], peer(step))
+
+    def send_last(i):
+        for source in range(3):
+            @pl.when(chip == source)
+            def _():
+                for step in range(3 - source, 0, -1):
+                    last_copy(source, i, step).start()
+
+    def half_rows(i):
+        return pl.ds(pl.multiple_of(row0 + ((NCH - 1) * DUO + i) * CH, CH), CH)
+
+    def base_copy(i):
+        return remote(base_out.at[half_rows(i)], base_out.at[half_rows(i)], base_send.at[i], base_recv.at[i], sibling)
+
+    def take_last(i):
+        for mine in range(4):
+            @pl.when(chip == mine)
+            def _():
+                value = x_own[NCH - 1, i]
+                for source in range(mine):
+                    last_copy(source, i, 1).wait_recv()
+                    value = value + rec_last[source, i]
+                base_out[half_rows(i), :] = value
+                base_copy(i).start()
 
     def send_local(e):
         c = lax.rem(e, NCH)
@@ -173,54 +212,68 @@
     def local_copy(c):
         return remote(loc.at[pl.ds((1 - core) * STEPS, STEPS), c], loc_out.at[:, core * NCH + c], out_send.at[0, c], out_recv.at[0, c], sibling)
 
+    def one_block(i, c, c_after, event):
+        follow = (i + 1) % DUO
+        stage_x(follow, c_after)
+        f_c = f_u = None
+        for n in range(4):
+            weight = w_out[256 * n:256 * n + 256, :]
+            cond, free = gelus(i, n)
+            part_c, part_u = dot(cond, weight), dot(free, weight)
+            f_c = part_c if n == 0 else f_c + part_c
+            f_u = part_u if n == 0 else f_u + part_u
+            if n == 1:
+                stage_a(follow)
+        stage_f(i, c, event, f_c, f_u)
+
     def one_round(r, carry):
         c = lax.rem(r, NCH)
-        c_next = lax.rem(r + 1, NCH)
 
         @pl.when(r >= 1)
         def _():
             send_sum(r - 1)
 
-        @pl.when((r >= NEED) & (r < NEED + NB - NCH))
+        @pl.when((r >= PASS) & (r < PASS + NB - NCH))
+        def _():
+            relay(r - PASS, False)
+
+        @pl.when(r >= PASS + NB - NCH)
+        def _():
+            relay(r - PASS, True)
+
+        @pl.when(r >= NEED)
         def _():
             take(r - NEED, False)
 
-        @pl.when(r >= NEED + NB - NCH)
-        def _():
-            take(r - NEED, True)
-
         @pl.when(r >= NB - NCH + 1)
         def _():
             send_local(r - 1)
 
-        for i in range(DUO):
-            follow = (i + 1) % DUO
-            stage_x(follow, c if i + 1 < DUO else c_next)
-            f_c = f_u = None
-            for n in range(4):
-                weight = w_out[256 * n:256 * n + 256, :]
-                cond, free = gelus(i, n)
-                part_c, part_u = dot(cond, weight), dot(free, weight)
-                f_c = part_c if n == 0 else f_c + part_c
-                f_u = part_u if n == 0 else f_u + part_u
-                if n == 1:
-                    stage_a(follow)
-            stage_f(i, c, r, f_c, f_u)
+        one_block(0, c, c, r)
+        one_block(1, c, lax.rem(r + 1, NCH), r)
         return carry
 
-    stage_x(0, 0)
-    stage_a(0)
-    lax.fori_loop(0, NB, one_round, 0)
-    send_sum(NB - 1)
-    send_local(NB - 1)
+    lax.fori_loop(0, NB - 1, one_round, 0)
+    send_sum(NB - 2)
+    relay(NB - 1 - PASS, True)
+    take(NB - 1 - NEED, True)
+    send_local(NB - 2)
 
     @pl.when(chip == 0)
     def _():
-        for c in range(NCH):
+        for c in range(NCH - 1):
             set_base(c, None, True)
 
-    for e in range(NB - NEED, NB):
+    one_block(0, NCH - 1, NCH - 1, NB - 1)
+    send_last(0)
+    one_block(1, NCH - 1, 0, NB - 1)
+    send_last(1)
+    send_local(NB - 1)
+    relay(NB - 2, True)
+    for e in range(NB - NEED, NB - 1):
         take(e, True)
+    take_last(0)
+    take_last(1)
 
     def drain(e, carry):
         @pl.when((chip == 0) | (chip == 2))
@@ -233,19 +286,33 @@
             copy_to(0, e, vbuf.at[e], 2).wait_send()
         return carry
 
-    def finish_out(c, carry):
+    def finish_local(c, carry):
+        local_copy(c).wait()
+        return carry
+
+    def finish_base(c, carry):
         rows = round_rows(c)
-        local_copy(c).wait()
         remote(base_out.at[rows], base_out.at[rows], out_send.at[1, c], out_recv.at[1, c], sibling).wait()
         return carry
 
-    lax.fori_loop(0, NB, drain, 0)
-    lax.fori_loop(0, NCH, finish_out, 0)
+    lax.fori_loop(0, NB - 1, drain, 0)
+    for source in range(3):
+        @pl.when(chip == source)
+        def _():
+            for i in range(DUO):
+                for step in range(1, 4 - source):
+                    last_copy(source, i, step).wait_send()
+
+    lax.fori_loop(0, NCH, finish_local, 0)
+    lax.fori_loop(0, NCH - 1, finish_base, 0)
+    base_copy(0).wait()
+    base_copy(1).wait()
 
 
 def solution(mesh):
     vmem = pl.BlockSpec(memory_space=pltpu.VMEM)
     smem = pl.BlockSpec(memory_space=pltpu.SMEM)
+    hbm = pl.BlockSpec(memory_space=pltpu.HBM)
     dma = pltpu.SemaphoreType.DMA
 
     def local(x_init, w_in, w_out, gamma_c, beta_c, gamma_u, beta_u, step_h, guide_w):
@@ -254,13 +321,16 @@
         loc, base = pl.pallas_call(
             kernel,
             out_shape=(jax.ShapeDtypeStruct((STEPS, 2 * NCH, DUO, CH, width), jnp.float32), jax.ShapeDtypeStruct((rows, width), jnp.float32)),
-            in_specs=[vmem] * 7 + [smem] * 2,
+            in_specs=[hbm] * 7 + [smem] * 2,
             out_specs=(vmem, vmem),
             scratch_shapes=[
+                pltpu.VMEM((NCH, DUO, CH, WIDTH), jnp.float32),
+                pltpu.VMEM((HIDDEN, WIDTH), jnp.bfloat16),
                 pltpu.VMEM((PAIR, NCH, DUO, CH, WIDTH), jnp.float32),
                 pltpu.VMEM((NCH, DUO, CH, WIDTH), jnp.float32),
                 pltpu.VMEM((PAIR, 4, 8, HIDDEN), jnp.float32),
                 pltpu.VMEM((PAIR, 8, 128), jnp.float32),
+                pltpu.VMEM((4, STEPS, HIDDEN), jnp.bfloat16),
                 pltpu.VMEM((4, STEPS, HIDDEN), jnp.bfloat16),
                 pltpu.VMEM((4, WIDTH, WIDTH), jnp.bfloat16),
                 pltpu.VMEM((DUO, ROWS, WIDTH), jnp.bfloat16),
@@ -268,11 +338,13 @@
                 pltpu.VMEM((NB, DUO, CH, WIDTH), jnp.float32),
                 pltpu.VMEM((NB, DUO, CH, WIDTH), jnp.float32),
                 pltpu.VMEM((2, NB, DUO, CH, WIDTH), jnp.float32),
-                dma((5,)), dma((5,)), dma((2, NB)), dma((2, NB)), dma((2, NCH)), dma((2, NCH)),
+                pltpu.VMEM((3, DUO, CH, WIDTH), jnp.float32),
+                dma((10,)), dma((5,)), dma((5,)), dma((2, NB - 1)), dma((2, NB - 1)), dma((2, NCH)), dma((2, NCH)),
+                dma((3, DUO)), dma((3, DUO)), dma((DUO,)), dma((DUO,)),
             ],
             compiler_params=pltpu.CompilerParams(collective_id=0, has_side_effects=True, vmem_limit_bytes=48 * 2 ** 20),
             name="picard",
-        )(x_init.reshape(rows, width), w_in, w_out, gamma_c, beta_c, gamma_u, beta_u, step_h, guide_w)
+        )(*(pltpu.with_memory_space_constraint(value, pltpu.HBM) for value in (x_init.reshape(2, NCH, DUO, CH, width), w_in, w_out, gamma_c, beta_c, gamma_u, beta_u)), step_h, guide_w)
         return (base[None] + loc.reshape(STEPS, rows, width)).reshape(STEPS, samples, tokens, width)
 
     return jax.shard_map(local, mesh=mesh, in_specs=(P("data", None, None), P(None, None), P(None, None), P("time", None), P("time", None), P("time", None), P("time", None), P("time"), P(None)), out_specs=P("time", "data", None, None), check_vma=False)

time: 61.7 us -> 54.4 us (0.88)
  local copies, waits for them, and re-layouts: 6.64 us -> 0.65 us
  Pallas kernels: 51.8 us -> 50.8 us
    unnamed x16 -> x2, local copies, waits for them, and re-layouts: 6.64 us -> 0.65 us
    pallas_call x1, Pallas kernels: 51.8 us -> 50.8 us  [local(): pl.pallas_call(kernel, out_shape=(jax.ShapeDtypeStruct((STEPS, 2 * NCH, D...]
where the time goes in v2:
time: 54.4 us; the launch traced here: 54.2 us
  Pallas kernels  50.8 us (93%)
  other arithmetic  2.09 us (4%)
  between operations  0.67 us (1%)
  local copies, waits for them, and re-layouts  0.65 us (1%)
    pallas_call x1, Pallas kernels, local(): pl.pallas_call(kernel, out_shape=(jax.ShapeDtypeStruct((STEPS, 2 * NCH, D...  50.8 us
    add x1, other arithmetic, local(): base[None] + loc.reshape(STEPS, rows, width)  2.09 us

profile of v2, /device:TPU:5, one launch (start us, length us, event | category | flops | bytes accessed | tf_op | source)
XLA Modules:
  0.0 54.2 jit_solution(9257679722862194484)
XLA Ops:
  0.7 0.0 copy-start
  0.7 0.6 %copy-done = f32[6]{0:T(128)S(1)} copy-done((f32[6]{0:T(128)S(1)}, f32[6]{0:T(128)}, u32[]{:S(2)}) %copy-start) | copy-done | bytes 48
  1.3 50.8 %picard.1 = (f32[6,8,2,32,256]{4,3,2,1,0:T(8,128)S(1)}, f32[512,256]{1,0:T(8,128)S(1)}) custom-call(f32[2,4,2,32,256]{4,3,2,1,0:T(8,128)} %bitcast.5, bf16[256,1024]{1,0:T(8,128)(2,1)} %w_in.1, bf16[1024,256]{1,0:T(8,128)(2,1)} %w_out_hbm.1, bf16[6,1024]{1,0:T(8,128)(2,1)} %gamma_c.1, bf16[6,1024]{1,0:T(8,128)(2,1)} %beta_c.1, bf16[6,1024]{1,0:T(8,128)(2,1)} %gamma_u.1, ...), custom_call_target="tpu_custom_call" | custom-call | tf_op jit(solution)/shard_map/picard/pallas_call | solution.py:321
  52.1 2.1 %broadcast_add_fusion = f32[6,32,16,256]{3,2,1,0:T(8,128)} fusion(f32[6,32,16,256]{3,2,1,0:T(8,128)S(1)} %bitcast.3, f32[32,16,256]{2,1,0:T(8,128)S(1)} %bitcast.4), kind=kLoop, calls=%fused_computation | loop fusion | flops 786432 | bytes 6815744 | tf_op jit(solution)/shard_map/add | solution.py:348
Async XLA Ops:
  0.7 0.7 %copy-start = (f32[6]{0:T(128)S(1)}, f32[6]{0:T(128)}, u32[]{:S(2)}) copy-start(f32[6]{0:T(128)} %h_ref.1) | copy-start | bytes 76

commit v3 on v2

--- a/solution.py
+++ b/solution.py
@@ -10,8 +10,8 @@
 
 NUM_SWEEPS = 4
 ROOT = math.sqrt(2.0 / math.pi)
-LIN = 2.0 * ROOT
-CUB = 8.0 * ROOT * 0.044715
+SCALE = (ROOT * 0.044715) ** (1.0 / 3.0)
+LIN = ROOT / SCALE
 CH = 32
 DUO = 2
 NCH = 4
@@ -24,18 +24,18 @@
 HIDDEN = 1024
 NEED = 3
 PASS = 2
+AHEAD = ({0: (0,), 1: (1,), 2: (2,), 3: (3,)}, {0: (0,), 1: (1,), 2: (2,), 3: (3,)})
 MESH = pl.DeviceIdType.MESH
 
 dot = functools.partial(jnp.dot, preferred_element_type=jnp.float32)
 
 
-def half_gelu(pre, gain, shift):
-    half = pre * gain + shift
-    arg = half * (half * half * CUB + LIN)
-    return (half * (1.0 + jnp.tanh(arg))).astype(jnp.bfloat16)
-
-
-def kernel(x_hbm, w_in, w_out_hbm, gamma_c, beta_c, gamma_u, beta_u, h_ref, guide_ref, loc_out, base_out, x_own, w_out, loc, base, par, hvec, own_par,
+def scaled_gelu(pre, gain, shift):
+    y = pre * gain + shift
+    return (y * (1.0 + jnp.tanh(y * (y * y + LIN)))).astype(jnp.bfloat16)
+
+
+def kernel(x_hbm, w_in, w_out_hbm, gamma_c, beta_c, gamma_u, beta_u, h_hbm, guide_ref, loc_out, base_out, h_ref, x_own, w_out, loc, base, par, hvec, own_par,
            sib_par, w1, xb, abuf, tbuf, vbuf, rec, rec_last, in_sem, sib_send, sib_recv, send_sem, recv_sem, out_send, out_recv, last_send, last_recv,
            base_send, base_recv):
     time = lax.axis_index("time")
@@ -49,7 +49,7 @@
         return lax.rem(time + 2 * step, 8)
 
     raw = [gamma_c, beta_c, gamma_u, beta_u]
-    pairs = [(raw[i], own_par.at[i]) for i in range(4)] + [(x_hbm.at[core], x_own)]
+    pairs = [(raw[i], own_par.at[i]) for i in range(4)] + [(h_hbm, h_ref), (x_hbm.at[core], x_own)]
     pairs += [(w_in.at[:, pl.ds(256 * n, 256)], w1.at[n]) for n in range(4)] + [(w_out_hbm, w_out)]
     fetches = [pltpu.make_async_copy(src, dst, in_sem.at[i]) for i, (src, dst) in enumerate(pairs)]
     for fetch in fetches:
@@ -64,10 +64,10 @@
         return pltpu.make_async_remote_copy(src_ref=src, dst_ref=dst, send_sem=send, recv_sem=recv, device_id=(data, target), device_id_type=MESH)
 
     own = pl.ds(core * STEPS, STEPS)
+    for fetch in fetches[:5]:
+        fetch.wait()
     for k in range(STEPS):
-        hvec[core * STEPS + k] = jnp.full((8, 128), h_ref[k], jnp.float32)
-    for fetch in fetches[:4]:
-        fetch.wait()
+        hvec[core * STEPS + k] = jnp.full((8, 128), h_ref[k] * (0.5 / SCALE), jnp.float32)
     par_copies = [remote(own_par.at[i], sib_par.at[i], sib_send.at[i], sib_recv.at[i], sibling) for i in range(4)]
     par_copies.append(remote(hvec.at[own], hvec.at[own], sib_send.at[4], sib_recv.at[4], sibling))
     for copy in par_copies:
@@ -76,7 +76,7 @@
     def spread(refs, first):
         for i in range(4):
             full = refs[i][...].astype(jnp.float32)
-            full = 0.5 * (1.0 + full) if i % 2 == 0 else 0.5 * full
+            full = SCALE * (1.0 + full) if i % 2 == 0 else SCALE * full
             for k in range(STEPS):
                 par[first + k, i] = jnp.broadcast_to(full[k:k + 1], (8, HIDDEN))
 
@@ -88,13 +88,13 @@
             value = base[c, i] if t == 0 else base[c, i] + loc[t, c, i]
             xb[i, CH * t:CH * t + CH, :] = value.astype(jnp.bfloat16)
 
-    def stage_a(i):
-        for n in range(4):
+    def stage_a(i, tiles=range(4)):
+        for n in tiles:
             abuf[i, n] = dot(xb[i], w1[n])
 
     loc[...] = jnp.zeros_like(loc)
     spread([own_par.at[i] for i in range(4)], core * STEPS)
-    for fetch in fetches[4:]:
+    for fetch in fetches[5:]:
         fetch.wait()
     base[...] = x_own[...]
     stage_x(0, 0)
@@ -111,8 +111,8 @@
         for t in range(PAIR):
             wide = [jnp.concatenate([par[t, p, :, lanes]] * (CH // 8), axis=0) for p in range(4)]
             pre = abuf[i, n, CH * t:CH * t + CH, :]
-            cond.append(half_gelu(pre, wide[0], wide[1]))
-            free.append(half_gelu(pre, wide[2], wide[3]))
+            cond.append(scaled_gelu(pre, wide[0], wide[1]))
+            free.append(scaled_gelu(pre, wide[2], wide[3]))
         return jnp.concatenate(cond, axis=0), jnp.concatenate(free, axis=0)
 
     def stage_f(i, c, event, f_c, f_u):
@@ -222,8 +222,8 @@
             part_c, part_u = dot(cond, weight), dot(free, weight)
             f_c = part_c if n == 0 else f_c + part_c
             f_u = part_u if n == 0 else f_u + part_u
-            if n == 1:
-                stage_a(follow)
+            if n in AHEAD[i]:
+                stage_a(follow, AHEAD[i][n])
         stage_f(i, c, event, f_c, f_u)
 
     def one_round(r, carry):
@@ -321,9 +321,10 @@
         loc, base = pl.pallas_call(
             kernel,
             out_shape=(jax.ShapeDtypeStruct((STEPS, 2 * NCH, DUO, CH, width), jnp.float32), jax.ShapeDtypeStruct((rows, width), jnp.float32)),
-            in_specs=[hbm] * 7 + [smem] * 2,
+            in_specs=[hbm] * 8 + [smem],
             out_specs=(vmem, vmem),
             scratch_shapes=[
+                pltpu.SMEM((STEPS,), jnp.float32),
                 pltpu.VMEM((NCH, DUO, CH, WIDTH), jnp.float32),
                 pltpu.VMEM((HIDDEN, WIDTH), jnp.bfloat16),
                 pltpu.VMEM((PAIR, NCH, DUO, CH, WIDTH), jnp.float32),
@@ -339,12 +340,12 @@
                 pltpu.VMEM((NB, DUO, CH, WIDTH), jnp.float32),
                 pltpu.VMEM((2, NB, DUO, CH, WIDTH), jnp.float32),
                 pltpu.VMEM((3, DUO, CH, WIDTH), jnp.float32),
-                dma((10,)), dma((5,)), dma((5,)), dma((2, NB - 1)), dma((2, NB - 1)), dma((2, NCH)), dma((2, NCH)),
+                dma((11,)), dma((5,)), dma((5,)), dma((2, NB - 1)), dma((2, NB - 1)), dma((2, NCH)), dma((2, NCH)),
                 dma((3, DUO)), dma((3, DUO)), dma((DUO,)), dma((DUO,)),
             ],
             compiler_params=pltpu.CompilerParams(collective_id=0, has_side_effects=True, vmem_limit_bytes=48 * 2 ** 20),
             name="picard",
-        )(*(pltpu.with_memory_space_constraint(value, pltpu.HBM) for value in (x_init.reshape(2, NCH, DUO, CH, width), w_in, w_out, gamma_c, beta_c, gamma_u, beta_u)), step_h, guide_w)
+        )(*(pltpu.with_memory_space_constraint(value, pltpu.HBM) for value in (x_init.reshape(2, NCH, DUO, CH, width), w_in, w_out, gamma_c, beta_c, gamma_u, beta_u, step_h)), guide_w)
         return (base[None] + loc.reshape(STEPS, rows, width)).reshape(STEPS, samples, tokens, width)
 
     return jax.shard_map(local, mesh=mesh, in_specs=(P("data", None, None), P(None, None), P(None, None), P("time", None), P("time", None), P("time", None), P("time", None), P("time"), P(None)), out_specs=P("time", "data", None, None), check_vma=False)

time: 54.4 us -> 49.4 us (0.908)
  Pallas kernels: 50.8 us -> 46.2 us
  local copies, waits for them, and re-layouts: 0.65 us -> 0 us
    pallas_call x1, Pallas kernels: 50.8 us -> 46.2 us  [local(): pl.pallas_call(kernel, out_shape=(jax.ShapeDtypeStruct((STEPS, 2 * NCH, D...]
    unnamed x2 -> x0, local copies, waits for them, and re-layouts: 0.65 us -> none
where the time goes in v3:
time: 49.4 us; the launch traced here: 49.2 us
  Pallas kernels  46.2 us (94%)
  other arithmetic  2.37 us (5%)
  between operations  0.66 us (1%)
    pallas_call x1, Pallas kernels, local(): pl.pallas_call(kernel, out_shape=(jax.ShapeDtypeStruct((STEPS, 2 * NCH, D...  46.2 us
    add x1, other arithmetic, local(): base[None] + loc.reshape(STEPS, rows, width)  2.37 us

profile of v3, /device:TPU:5, one launch (start us, length us, event | category | flops | bytes accessed | tf_op | source)
XLA Modules:
  0.0 49.2 jit_solution(14900681387429578248)
XLA Ops:
  0.7 46.2 %picard.1 = (f32[6,8,2,32,256]{4,3,2,1,0:T(8,128)S(1)}, f32[512,256]{1,0:T(8,128)S(1)}) custom-call(f32[2,4,2,32,256]{4,3,2,1,0:T(8,128)} %bitcast.5, bf16[256,1024]{1,0:T(8,128)(2,1)} %w_in.1, bf16[1024,256]{1,0:T(8,128)(2,1)} %w_out_hbm.1, bf16[6,1024]{1,0:T(8,128)(2,1)} %gamma_c.1, bf16[6,1024]{1,0:T(8,128)(2,1)} %beta_c.1, bf16[6,1024]{1,0:T(8,128)(2,1)} %gamma_u.1, ...), custom_call_target="tpu_custom_call" | custom-call | tf_op jit(solution)/shard_map/picard/pallas_call | solution.py:321
  46.9 2.4 %broadcast_add_fusion = f32[6,32,16,256]{3,2,1,0:T(8,128)} fusion(f32[6,32,16,256]{3,2,1,0:T(8,128)S(1)} %bitcast.3, f32[32,16,256]{2,1,0:T(8,128)S(1)} %bitcast.4), kind=kLoop, calls=%fused_computation | loop fusion | flops 786432 | bytes 6815744 | tf_op jit(solution)/shard_map/add | solution.py:349

commit v4 on v3

--- a/solution.py
+++ b/solution.py
@@ -21,10 +21,11 @@
 PAIR = 2 * STEPS
 ROWS = PAIR * CH
 WIDTH = 256
+PIECES = 8
 HIDDEN = 1024
 NEED = 3
 PASS = 2
-AHEAD = ({0: (0,), 1: (1,), 2: (2,), 3: (3,)}, {0: (0,), 1: (1,), 2: (2,), 3: (3,)})
+AHEAD = ({1: (0,), 2: (1, 2), 3: (3,)}, {1: (0,), 2: (1, 2), 3: (3,)})
 MESH = pl.DeviceIdType.MESH
 
 dot = functools.partial(jnp.dot, preferred_element_type=jnp.float32)
@@ -307,6 +308,18 @@
     lax.fori_loop(0, NCH - 1, finish_base, 0)
     base_copy(0).wait()
     base_copy(1).wait()
+
+
+def finish(loc_ref, base_ref, out_hbm, stage, sem):
+    pieces = []
+    for piece in range(PIECES):
+        rows = pl.ds(piece * (2 * OWN // PIECES), 2 * OWN // PIECES)
+        for k in range(STEPS):
+            stage[k, rows, :] = base_ref[rows, :] + loc_ref[k, rows, :]
+        pieces.append(pltpu.make_async_copy(stage.at[:, rows], out_hbm.at[:, rows], sem.at[piece]))
+        pieces[-1].start()
+    for copy in pieces:
+        copy.wait()
 
 
 def solution(mesh):
@@ -346,6 +359,15 @@
             compiler_params=pltpu.CompilerParams(collective_id=0, has_side_effects=True, vmem_limit_bytes=48 * 2 ** 20),
             name="picard",
         )(*(pltpu.with_memory_space_constraint(value, pltpu.HBM) for value in (x_init.reshape(2, NCH, DUO, CH, width), w_in, w_out, gamma_c, beta_c, gamma_u, beta_u, step_h)), guide_w)
-        return (base[None] + loc.reshape(STEPS, rows, width)).reshape(STEPS, samples, tokens, width)
+        out = pl.pallas_call(
+            finish,
+            out_shape=jax.ShapeDtypeStruct((STEPS, rows, width), jnp.float32),
+            in_specs=[vmem] * 2,
+            out_specs=hbm,
+            scratch_shapes=[pltpu.VMEM((STEPS, rows, width), jnp.float32), dma((PIECES,))],
+            compiler_params=pltpu.CompilerParams(vmem_limit_bytes=8 * 2 ** 20),
+            name="finish",
+        )(loc.reshape(STEPS, rows, width), base)
+        return out.reshape(STEPS, samples, tokens, width)
 
     return jax.shard_map(local, mesh=mesh, in_specs=(P("data", None, None), P(None, None), P(None, None), P("time", None), P("time", None), P("time", None), P("time", None), P("time"), P(None)), out_specs=P("time", "data", None, None), check_vma=False)

time: 49.4 us -> 48 us (0.972)
  other arithmetic: 2.37 us -> 0 us
  Pallas kernels: 46.2 us -> 47.2 us
    add x1 -> x0, other arithmetic: 2.37 us -> none  [local(): base[None] + loc.reshape(STEPS, rows, width)]
    pallas_call x0 -> x1, Pallas kernels: none -> 1.75 us  [local(): pl.pallas_call(finish, out_shape=jax.ShapeDtypeStruct((STEPS, rows, width...]
    pallas_call x1, Pallas kernels: 46.2 us -> 45.4 us  [local(): pl.pallas_call(kernel, out_shape=(jax.ShapeDtypeStruct((STEPS, 2 * NCH, D...]
where the time goes in v4:
time: 48 us; the launch traced here: 47.9 us
  Pallas kernels  47.2 us (98%)
  between operations  0.66 us (1%)
    pallas_call x1, Pallas kernels, local(): pl.pallas_call(kernel, out_shape=(jax.ShapeDtypeStruct((STEPS, 2 * NCH, D...  45.4 us
    pallas_call x1, Pallas kernels, local(): pl.pallas_call(finish, out_shape=jax.ShapeDtypeStruct((STEPS, rows, width...  1.75 us

profile of v4, /device:TPU:5, one launch (start us, length us, event | category | flops | bytes accessed | tf_op | source)
XLA Modules:
  0.0 47.9 jit_solution(8142765457865049407)
XLA Ops:
  0.7 45.4 %picard.1 = (f32[6,8,2,32,256]{4,3,2,1,0:T(8,128)S(1)}, f32[512,256]{1,0:T(8,128)S(1)}) custom-call(f32[2,4,2,32,256]{4,3,2,1,0:T(8,128)} %bitcast.4, bf16[256,1024]{1,0:T(8,128)(2,1)} %w_in.1, bf16[1024,256]{1,0:T(8,128)(2,1)} %w_out_hbm.1, bf16[6,1024]{1,0:T(8,128)(2,1)} %gamma_c.1, bf16[6,1024]{1,0:T(8,128)(2,1)} %beta_c.1, bf16[6,1024]{1,0:T(8,128)(2,1)} %gamma_u.1, ...), custom_call_target="tpu_custom_call" | custom-call | tf_op jit(solution)/shard_map/picard/pallas_call | solution.py:334
  46.1 1.8 %finish.1 = f32[6,512,256]{2,1,0:T(8,128)} custom-call(f32[6,512,256]{2,1,0:T(8,128)S(1)} %bitcast.3, f32[512,256]{1,0:T(8,128)S(1)} %get-tuple-element.8.base_ref), custom_call_target="tpu_custom_call" | custom-call | tf_op jit(solution)/shard_map/finish/pallas_call | solution.py:362

commit v5 on v4

--- a/solution.py
+++ b/solution.py
@@ -37,8 +37,8 @@
 
 
 def kernel(x_hbm, w_in, w_out_hbm, gamma_c, beta_c, gamma_u, beta_u, h_hbm, guide_ref, loc_out, base_out, h_ref, x_own, w_out, loc, base, par, hvec, own_par,
-           sib_par, w1, xb, abuf, tbuf, vbuf, rec, rec_last, in_sem, sib_send, sib_recv, send_sem, recv_sem, out_send, out_recv, last_send, last_recv,
-           base_send, base_recv):
+           sib_par, w1, xb, abuf, tbuf, vbuf, rec, rec_early, rec_last, in_sem, sib_send, sib_recv, send_sem, recv_sem, out_send, out_recv, last_send, last_recv,
+           base_send, base_recv, early_send, early_recv):
     time = lax.axis_index("time")
     data = lax.axis_index("data")
     core = lax.rem(time, 2)
@@ -176,6 +176,38 @@
             got(0, e)
             got(1, e)
             set_base(e, rec[0, e] + rec[1, e], last)
+
+    def early_copy(source):
+        return remote(tbuf.at[NB - 2], rec_early.at[source], early_send.at[0], early_recv.at[source], peer(2 - source))
+
+    def send_early():
+        for source in range(2):
+            @pl.when(chip == source)
+            def _():
+                early_copy(source).start()
+
+    def relay_early():
+        e = NB - 2
+
+        @pl.when(chip == 1)
+        def _():
+            got(0, e)
+            below = rec[0, e]
+            vbuf[e] = below + tbuf[e]
+            copy_to(0, e, vbuf.at[e], 2).start()
+            set_base(e, below, True)
+
+        @pl.when(chip == 2)
+        def _():
+            for source in range(2):
+                early_copy(source).wait_recv()
+            set_base(e, rec_early[0] + rec_early[1], True)
+
+        @pl.when(chip == 3)
+        def _():
+            got(0, e)
+            got(1, e)
+            set_base(e, rec[0, e] + rec[1, e], True)
 
     def last_copy(source, i, step):
         return remote(tbuf.at[NB - 1, i], rec_last.at[source, i], last_send.at[step - 1, i], last_recv.at[source, i], peer(step))
@@ -256,6 +288,7 @@
 
     lax.fori_loop(0, NB - 1, one_round, 0)
     send_sum(NB - 2)
+    send_early()
     relay(NB - 1 - PASS, True)
     take(NB - 1 - NEED, True)
     send_local(NB - 2)
@@ -270,9 +303,9 @@
     one_block(1, NCH - 1, 0, NB - 1)
     send_last(1)
     send_local(NB - 1)
-    relay(NB - 2, True)
-    for e in range(NB - NEED, NB - 1):
+    for e in range(NB - NEED, NB - 2):
         take(e, True)
+    relay_early()
     take_last(0)
     take_last(1)
 
@@ -296,7 +329,20 @@
         remote(base_out.at[rows], base_out.at[rows], out_send.at[1, c], out_recv.at[1, c], sibling).wait()
         return carry
 
-    lax.fori_loop(0, NB - 1, drain, 0)
+    lax.fori_loop(0, NB - 2, drain, 0)
+
+    @pl.when((chip == 0) | (chip == 2))
+    def _():
+        copy_to(0, NB - 2, tbuf.at[NB - 2], 1).wait_send()
+
+    @pl.when(chip == 1)
+    def _():
+        copy_to(0, NB - 2, vbuf.at[NB - 2], 2).wait_send()
+
+    @pl.when(chip < 2)
+    def _():
+        early_copy(0).wait_send()
+
     for source in range(3):
         @pl.when(chip == source)
         def _():
@@ -352,9 +398,10 @@
                 pltpu.VMEM((NB, DUO, CH, WIDTH), jnp.float32),
                 pltpu.VMEM((NB, DUO, CH, WIDTH), jnp.float32),
                 pltpu.VMEM((2, NB, DUO, CH, WIDTH), jnp.float32),
+                pltpu.VMEM((2, DUO, CH, WIDTH), jnp.float32),
                 pltpu.VMEM((3, DUO, CH, WIDTH), jnp.float32),
                 dma((11,)), dma((5,)), dma((5,)), dma((2, NB - 1)), dma((2, NB - 1)), dma((2, NCH)), dma((2, NCH)),
-                dma((3, DUO)), dma((3, DUO)), dma((DUO,)), dma((DUO,)),
+                dma((3, DUO)), dma((3, DUO)), dma((DUO,)), dma((DUO,)), dma((1,)), dma((2,)),
             ],
             compiler_params=pltpu.CompilerParams(collective_id=0, has_side_effects=True, vmem_limit_bytes=48 * 2 ** 20),
             name="picard",

time: 48 us -> 49.3 us (1.027)
  Pallas kernels: 47.2 us -> 48.4 us
    pallas_call x1, Pallas kernels: 45.4 us -> 46.7 us  [local(): pl.pallas_call(kernel, out_shape=(jax.ShapeDtypeStruct((STEPS, 2 * NCH, D...]
where the time goes in v5:
time: 49.3 us; the launch traced here: 49.1 us
  Pallas kernels  48.4 us (98%)
  between operations  0.66 us (1%)
    pallas_call x1, Pallas kernels, local(): pl.pallas_call(kernel, out_shape=(jax.ShapeDtypeStruct((STEPS, 2 * NCH, D...  46.7 us
    pallas_call x1, Pallas kernels, local(): pl.pallas_call(finish, out_shape=jax.ShapeDtypeStruct((STEPS, rows, width...  1.75 us

profile of v5, /device:TPU:5, one launch (start us, length us, event | category | flops | bytes accessed | tf_op | source)
XLA Modules:
  0.0 49.1 jit_solution(5020165782324390174)
XLA Ops:
  0.7 46.7 %picard.1 = (f32[6,8,2,32,256]{4,3,2,1,0:T(8,128)S(1)}, f32[512,256]{1,0:T(8,128)S(1)}) custom-call(f32[2,4,2,32,256]{4,3,2,1,0:T(8,128)} %bitcast.4, bf16[256,1024]{1,0:T(8,128)(2,1)} %w_in.1, bf16[1024,256]{1,0:T(8,128)(2,1)} %w_out_hbm.1, bf16[6,1024]{1,0:T(8,128)(2,1)} %gamma_c.1, bf16[6,1024]{1,0:T(8,128)(2,1)} %beta_c.1, bf16[6,1024]{1,0:T(8,128)(2,1)} %gamma_u.1, ...), custom_call_target="tpu_custom_call" | custom-call | tf_op jit(solution)/shard_map/picard/pallas_call | solution.py:380
  47.4 1.8 %finish.1 = f32[6,512,256]{2,1,0:T(8,128)} custom-call(f32[6,512,256]{2,1,0:T(8,128)S(1)} %bitcast.3, f32[512,256]{1,0:T(8,128)S(1)} %get-tuple-element.8.base_ref), custom_call_target="tpu_custom_call" | custom-call | tf_op jit(solution)/shard_map/finish/pallas_call | solution.py:409
